TPU v7x, 256 devices: a whole 4x4x8 slice. The times are simulated.
256 devices in a mesh: dp: 32 (over z_hi, y, core), tensor: 8 (over z_lo, x).
Axes of the slice: x: 4, y: 4, z: 8 (z_hi: 4, z_lo: 2; z = z_hi * 2 + z_lo), core: 2. Of those that a mesh axis runs over, the one named last changes fastest.
Arguments:
- tokens: bfloat16 [8192, 2560], P('dp'), may hold values from -6 to 6
- target: bfloat16 [8192, 2560], P('dp'), may hold values from -6 to 6
- norm_gain: float32 [2560], replicated, may hold values from 0.25 to 1.75
- gate_weight: bfloat16 [2560, 7168], P('dp', 'tensor'), may hold values from -0.125 to 0.125
- up_weight: bfloat16 [2560, 7168], P('dp', 'tensor'), may hold values from -0.125 to 0.125
- down_weight: bfloat16 [7168, 2560], P('tensor', 'dp'), may hold values from -0.0625 to 0.0625
- tangent: bfloat16 [2560, 7168], P('dp', 'tensor'), may hold values from -0.125 to 0.125
- lengths: int32 [4], replicated, may hold values from 512 to 2048
- loss_scale: float32 [1], replicated, may hold values from 16 to 64
Outputs:
- hvp: float32 [2560, 7168], P('dp', 'tensor')
- rayleigh: float32 [1], replicated
All inputs are finite; a program needn't handle non-finite values.
Results may differ from a plain program's by a relative error of at most 0.017.
Values may be sent and summed in bfloat16 or wider, within the bound.
No kernel may reach another device: no remote copies, remote signals or barrier semaphores. Data moves between devices by JAX's collectives and lax.ppermute only.
A program may use at most 128 MiB of HBM per device.

v0:
```python
import jax
import jax.numpy as jnp
from jax import lax
from jax.sharding import Mesh
from jax.sharding import PartitionSpec as P

DP = ("dp_0", "dp_1", "dp_2")
TENSOR = ("tensor_0", "tensor_1")
DP_TENSOR = ("dp_0", "dp_1", "dp_2", "tensor_0", "tensor_1")


def in_one_piece(arrays, axis, dim, along):
    both = jnp.concatenate(arrays, axis=along)
    filled, at, outs = (lax.all_gather(both, axis, axis=dim, tiled=True), 0, [])
    for a in arrays:
        outs.append(lax.slice_in_dim(filled, at, at + a.shape[along], axis=along))
        at += a.shape[along]
    return tuple(outs)


def one_axis_at_a_time(value, axes):
    for axis in axes:
        value = lax.psum(value, axis)
    return value


def token_weights(first_pos, row_total, micro_len, lengths, loss_scale):
    position = first_pos + jnp.arange(row_total, dtype=jnp.int32)
    micro_id = position // micro_len
    offset = position - micro_id * micro_len
    onehot = micro_id[:, None] == jnp.arange(lengths.shape[0], dtype=jnp.int32)[None, :]
    live_len = jnp.sum(jnp.where(onehot, lengths[None, :], 0), axis=1)
    return jnp.where(
        offset < live_len, loss_scale[0] / live_len.astype(jnp.float32), jnp.float32(0.0)
    )


def shards(
    tokens, target, norm_gain, gate_weight, up_weight, down_weight, tangent, lengths, loss_scale
):
    row_count = tokens.shape[0]
    stream = tokens.astype(jnp.float32)
    mean_sq = jnp.mean(stream * stream, axis=-1, keepdims=True)
    normed = (stream * lax.rsqrt(mean_sq + 1e-06) * norm_gain[None, :]).astype(jnp.bfloat16)
    pieces = in_one_piece((gate_weight, up_weight, tangent), DP, 0, 1)
    columns = normed
    gate_pre, up_pre, gate_tan = tuple(
        (jnp.dot(columns, piece, preferred_element_type=jnp.float32) for piece in pieces)
    )
    sigma = jax.nn.sigmoid(gate_pre)
    slope = sigma * (1.0 + gate_pre * (1.0 - sigma))
    bend = sigma * (1.0 - sigma) * (2.0 + gate_pre * (1.0 - 2.0 * sigma))
    hidden = (gate_pre * sigma * up_pre).astype(jnp.bfloat16)
    hidden_tan = (slope * gate_tan * up_pre).astype(jnp.bfloat16)
    down_full = lax.all_gather(down_weight, DP, axis=1, tiled=True)
    stacked = jnp.dot(
        jnp.concatenate([hidden, hidden_tan], axis=0), down_full, preferred_element_type=jnp.float32
    )
    branch = stacked[:row_count]
    branch_tan = stacked[row_count:]
    micro_len = row_count * lax.axis_size(DP) // lengths.shape[0]
    first_row = lax.axis_index(DP) * row_count
    branch, branch_tan = (
        lax.psum(branch.astype(jnp.bfloat16), TENSOR).astype(jnp.float32),
        lax.psum(branch_tan.astype(jnp.bfloat16), TENSOR).astype(jnp.float32),
    )
    weight = token_weights(first_row, row_count, micro_len, lengths, loss_scale)
    output = stream + branch
    grad_out = (weight[:, None] * (output - target.astype(jnp.float32))).astype(jnp.bfloat16)
    grad_tan = (weight[:, None] * branch_tan).astype(jnp.bfloat16)
    grads = lax.dot_general(
        jnp.concatenate([grad_out, grad_tan], axis=0),
        down_full,
        (((1,), (1,)), ((), ())),
        preferred_element_type=jnp.float32,
    )
    grad_hid = grads[:row_count]
    hess_hid = grads[row_count:]
    hess_pre = (hess_hid * up_pre * slope + grad_hid * up_pre * bend * gate_tan).astype(
        jnp.bfloat16
    )
    tangent_f = tangent.astype(jnp.float32)
    tangent_sq = jnp.sum(tangent_f * tangent_f)
    curvature, squares = (
        one_axis_at_a_time(jnp.sum(gate_tan * hess_pre.astype(jnp.float32)), DP_TENSOR),
        one_axis_at_a_time(tangent_sq, DP_TENSOR),
    )
    columns = normed
    product = lax.dot_general(
        columns, hess_pre, (((0,), (0,)), ((), ())), preferred_element_type=jnp.float32
    )
    hvp = lax.psum_scatter(
        lax.optimization_barrier(product.astype(jnp.bfloat16))
        .astype(jnp.float32)
        .astype(jnp.bfloat16),
        DP,
        scatter_dimension=0,
        tiled=True,
    ).astype(jnp.float32)
    rayleigh = (curvature / squares).reshape(1)
    return (hvp, rayleigh)


def solution(mesh):
    torus = Mesh(
        mesh.devices.reshape(4, 4, 2, 2, 4), ("dp_0", "dp_1", "dp_2", "tensor_0", "tensor_1")
    )
    return jax.shard_map(
        shards,
        mesh=torus,
        in_specs=(
            P(DP, None),
            P(DP, None),
            P(),
            P(DP, TENSOR),
            P(DP, TENSOR),
            P(TENSOR, DP),
            P(DP, TENSOR),
            P(),
            P(),
        ),
        out_specs=(P(DP, TENSOR), P()),
        check_vma=False,
    )
```

profile of v0, /device:TPU:2, one launch (start us, length us, event | category | flops | bytes accessed | tf_op | source)
XLA Modules:
  0.0 400.0 jit_solution(3529880794193507350)
XLA Ops:
  7.2 0.0 copy-start
  7.2 0.0 copy-start.7
  7.2 0.0 all-gather.3.cloned.1.call-start
  7.2 1.9 pad_maximum_fusion
  9.2 0.0 all-gather.3.cloned.1.call-update
  9.2 0.0 all-gather.5.cloned.1.call-start
  9.2 0.7 all-gather.5.cloned.1.call-update
  9.9 0.0 all-reduce.8.cloned.1.call-start
  10.0 1.7 fusion.6
  11.7 97.1 %all-gather.3.cloned.1.call-done = bf16[2560,2688]{1,0:T(8,128)(2,1)} async-done(((bf16[80,2688]{1,0:T(8,128)(2,1)}), bf16[2560,2688]{1,0:T(8,128)(2,1)}) %all-gather.3.cloned.1.call-update) | async-done | bytes 13762576 | tf_op jit(solution)/shard_map/all_gather | solution.py:14
  108.7 0.0 copy-done
  108.7 0.0 copy-done.7
  108.7 3.9 fusion
  112.6 3.9 fusion.4
  116.5 0.0 copy-start.2
  116.5 0.9 copy-done.2
  117.4 5.0 %multiply_convert_fusion.2 = (bf16[256,896]{1,0:T(8,128)(2,1)S(1)}, bf16[256,896]{1,0:T(8,128)(2,1)S(1)}, f32[256,896]{1,0:T(8,128)}) fusion(f32[256,896]{1,0:T(8,128)S(1)} %fusion.4, f32[256,896]{1,0:T(8,128)S(1)} %fusion, bf16[2560,2688]{1,0:T(8,128)(2,1)} %all-gather.3.cloned.1.call-done, bf16[256,2560]{1,0:T(8,128)(2,1)S(1)} %copy-done, ...), kind=kOutput, calls=%fused_computation.39 | convolution fusion | flops 1180008448 | bytes 9579520 | tf_op jit(solution)/shard_map/dot_general | solution.py:48
  122.4 58.1 %all-gather.5.cloned.1.call-done = bf16[896,2560]{0,1:T(8,128)(2,1)} async-done(((bf16[896,80]{0,1:T(8,128)(2,1)}), bf16[896,2560]{0,1:T(8,128)(2,1)}) %all-gather.5.cloned.1.call-update) | async-done | bytes 4587536 | tf_op jit(solution)/shard_map/all_gather | solution.py:55
  180.5 5.8 %convolution_convert_fusion.1 = bf16[512,2560]{1,0:T(8,128)(2,1)S(1)} fusion(bf16[896,2560]{0,1:T(8,128)(2,1)} %all-gather.5.cloned.1.call-done, bf16[256,896]{1,0:T(8,128)(2,1)S(1)} %get-tuple-element.19, bf16[256,896]{1,0:T(8,128)(2,1)S(1)} %get-tuple-element.18), kind=kOutput, calls=%fused_computation.7 | convolution fusion | flops 2351955968 | bytes 8126464 | tf_op jit(solution)/shard_map/dot_general | solution.py:56
  186.3 1.7 fusion.34
  188.0 0.0 copy-start.6
  188.0 0.0 copy-start.1
  188.0 0.0 all-reduce.8.cloned.1.call-update
  188.0 0.0 reduce-scatter.2.cloned.1.call-start
  188.8 0.0 copy-done.6
  188.9 0.1 select_reduce_fusion
  189.0 86.6 %all-reduce.8.cloned.1.call-done = (bf16[256,2560]{1,0:T(8,128)(2,1)}, bf16[256,2560]{1,0:T(8,128)(2,1)}) async-done(((bf16[256,2560]{1,0:T(8,128)(2,1)}, bf16[256,2560]{1,0:T(8,128)(2,1)}), (bf16[256,2560]{1,0:T(8,128)(2,1)}, bf16[256,2560]{1,0:T(8,128)(2,1)})) %all-reduce.8.cloned.1.call-update) | async-done | bytes 2621456 | tf_op jit(solution)/shard_map/psum | solution.py:65
  275.5 0.0 copy-done.1
  275.5 2.5 fusion.11
  278.1 0.0 copy-start.3
  278.1 0.0 copy-start.4
  278.1 5.3 %fusion.12 = f32[512,896]{1,0:T(8,128)S(1)} fusion(bf16[896,2560]{0,1:T(8,128)(2,1)} %all-gather.5.cloned.1.call-done, bf16[256,2560]{1,0:T(8,128)(2,1)S(1)} %get-tuple-element.21, bf16[256,2560]{1,0:T(8,128)(2,1)S(1)} %get-tuple-element.20), kind=kOutput, calls=%fused_computation.17 | convolution fusion | flops 2354053120 | bytes 9043968 | tf_op jit(solution)/shard_map/dot_general | solution.py:71
  283.4 0.0 copy-start.8
  283.4 0.0 copy-done.3
  283.4 0.0 copy-done.4
  283.4 1.3 multiply_reduce_fusion
  284.7 0.0 copy-done.8
  284.7 3.7 convolution_convert_fusion
  288.5 0.0 reduce-scatter.2.cloned.1.call-update
  288.5 0.9 copy-done.5
  289.4 0.7 multiply_reduce_fusion.1
  290.0 12.9 %all-reduce.2 = (f32[]{:T(128)}, f32[]{:T(128)}) all-reduce(f32[]{:T(128)} %get-tuple-element.14, f32[]{:T(128)} %multiply_reduce_fusion.1), channel_id=1, replica_groups=mesh['dp_0'=4,'dp_1'=4,'dp_2'=2,'tensor_0'=2,'tensor_1'=4] {'dp_0'}, use_global_device_ids=true, to_apply=%region_6.7 | all-reduce | flops 2 | bytes 16 | tf_op jit(solution)/shard_map/psum | solution.py:23
  302.9 11.1 %all-reduce.1 = (f32[]{:T(128)}, f32[]{:T(128)}) all-reduce(f32[]{:T(128)} %get-tuple-element.6, f32[]{:T(128)} %get-tuple-element.7), channel_id=1, replica_groups=mesh['dp_0'=4,'dp_1'=4,'dp_2'=2,'tensor_0'=2,'tensor_1'=4] {'dp_1'}, use_global_device_ids=true, to_apply=%region_7.8 | all-reduce | flops 2 | bytes 16 | tf_op jit(solution)/shard_map/psum | solution.py:23
  314.0 3.1 all-reduce.4
  317.1 5.5 %all-reduce.3 = (f32[]{:T(128)}, f32[]{:T(128)}) all-reduce(f32[]{:T(128)} %get-tuple-element.10, f32[]{:T(128)} %get-tuple-element.11), channel_id=1, replica_groups=mesh['dp_0'=4,'dp_1'=4,'dp_2'=2,'tensor_0'=2,'tensor_1'=4] {'tensor_0'}, use_global_device_ids=true, to_apply=%region_9.10 | all-reduce | flops 2 | bytes 16 | tf_op jit(solution)/shard_map/psum | solution.py:23
  322.6 9.6 %all-reduce = (f32[]{:T(128)}, f32[]{:T(128)}) all-reduce(f32[]{:T(128)} %get-tuple-element.8, f32[]{:T(128)} %get-tuple-element.9), channel_id=1, replica_groups=mesh['dp_0'=4,'dp_1'=4,'dp_2'=2,'tensor_0'=2,'tensor_1'=4] {'tensor_1'}, use_global_device_ids=true, to_apply=%region_10.11 | all-reduce | flops 2 | bytes 16 | tf_op jit(solution)/shard_map/psum | solution.py:23
  333.5 57.2 %reduce-scatter.2.cloned.1.call-done = bf16[80,896]{1,0:T(8,128)(2,1)} async-done(((bf16[2560,896]{1,0:T(8,128)(2,1)}), bf16[80,896]{1,0:T(8,128)(2,1)}) %reduce-scatter.2.cloned.1.call-update) | async-done | bytes 143376 | tf_op jit(solution)/shard_map/reduce_scatter | solution.py:92
  390.7 1.6 convert_element_type.65
  (4 shorter events, 0.0 us)
Async XLA Ops:
  7.2 101.6 %copy-start = (bf16[256,2560]{1,0:T(8,128)(2,1)S(1)}, bf16[256,2560]{1,0:T(8,128)(2,1)}, u32[]{:S(2)}) copy-start(bf16[256,2560]{1,0:T(8,128)(2,1)} %param.9) | copy-start | bytes 3932164
  7.2 101.6 %copy-start.7 = (f32[2560]{0:T(1024)S(1)}, f32[2560]{0:T(1024)}, u32[]{:S(2)}) copy-start(f32[2560]{0:T(1024)} %param.11) | copy-start | bytes 30724
  7.2 101.5 %all-gather.3.cloned.1.call-start = ((), (), s32[]{:S(2)}) async-start(), calls=%async_computation.1 | async-start | bytes 14192640 | tf_op jit(solution)/shard_map/all_gather | solution.py:14
  9.2 171.3 %all-gather.5.cloned.1.call-start = ((), (), s32[]{:S(2)}) async-start(), calls=%async_computation.2 | async-start | bytes 4730880 | tf_op jit(solution)/shard_map/all_gather | solution.py:55
  9.9 265.6 %all-reduce.8.cloned.1.call-start = ((), (), s32[]{:S(2)}) async-start(), calls=%async_computation.4 | async-start | bytes 5242880 | tf_op jit(solution)/shard_map/psum | solution.py:65
  116.5 0.9 copy-start.2
  188.0 0.8 copy-start.6
  188.0 87.5 %copy-start.1 = (bf16[256,2560]{1,0:T(8,128)(2,1)S(1)}, bf16[256,2560]{1,0:T(8,128)(2,1)}, u32[]{:S(2)}) copy-start(bf16[256,2560]{1,0:T(8,128)(2,1)} %param.10) | copy-start | bytes 3932164
  188.0 202.7 %reduce-scatter.2.cloned.1.call-start = ((), (), s32[]{:S(2)}) async-start(), calls=%async_computation.3 | async-start | bytes 4730880 | tf_op jit(solution)/shard_map/reduce_scatter | solution.py:92
  278.1 5.3 %copy-start.3 = (f32[256,896]{1,0:T(8,128)S(1)}, f32[256,896]{1,0:T(8,128)}, u32[]{:S(2)}) copy-start(f32[256,896]{1,0:T(8,128)} %copy-done.2) | copy-start | bytes 2752516
  278.1 5.3 %copy-start.4 = (f32[256,896]{1,0:T(8,128)S(1)}, f32[256,896]{1,0:T(8,128)}, u32[]{:S(2)}) copy-start(f32[256,896]{1,0:T(8,128)} %get-tuple-element.22) | copy-start | bytes 2752516
  283.4 1.3 copy-start.8
  288.4 0.9 copy-start.5
Sparse Core Ops, SparseCore 0:
  10.6 98.0 all-gather.2
  111.3 69.1 all-gather.4
  188.2 87.3 all-reduce.7
  288.6 102.0 reduce-scatter.1
where the time goes:
time: 401 us; the launch traced here: 400 us
  waiting for transfers between devices  300 us (75%)
  blocking collectives  42.1 us (10%)
  matrix products  27.5 us (7%)
  between operations  17.1 us (4%)
  other arithmetic  9.85 us (2%)
    all_gather x1, waiting for transfers between devices, in_one_piece(): filled, at, outs = (lax.all_gather(both, axis, axis=dim, tiled=True), 0, [])  97.1 us
    psum x1, waiting for transfers between devices, shards(): lax.psum(branch_tan.astype(jnp.bfloat16), TENSOR).astype(jnp.float32)  86.6 us
    all_gather x1, waiting for transfers between devices, shards(): down_full = lax.all_gather(down_weight, DP, axis=1, tiled=True)  58.1 us
    reduce_scatter x1, waiting for transfers between devices, shards(): lax.psum_scatter(lax.optimization_barrier(product.astype(jnp.bfloat16)).a...  57.2 us
    psum x5, blocking collectives, one_axis_at_a_time(): value = lax.psum(value, axis)  42.1 us
    dot_general x3, matrix products, shards(): jnp.dot(columns, piece, preferred_element_type=jnp.float32)  12.7 us
  transfers between devices with their start and end apart: 4, of which 4 were waited for; matrix products, arithmetic and copies ran while one was open for 4% of the time, Pallas kernels for 0%

commit v1 on v0

--- a/solution.py
+++ b/solution.py
@@ -52,7 +52,7 @@
     bend = sigma * (1.0 - sigma) * (2.0 + gate_pre * (1.0 - 2.0 * sigma))
     hidden = (gate_pre * sigma * up_pre).astype(jnp.bfloat16)
     hidden_tan = (slope * gate_tan * up_pre).astype(jnp.bfloat16)
-    down_full = lax.all_gather(down_weight, DP, axis=1, tiled=True)
+    down_full = jnp.concatenate(lax.all_gather(down_weight, axis_name=DP), axis=1)
     stacked = jnp.dot(
         jnp.concatenate([hidden, hidden_tan], axis=0), down_full, preferred_element_type=jnp.float32
     )

time: 401 us -> 411 us (1.025)
  waiting for transfers between devices: 300 us -> 306 us
  local copies, waits for them, and re-layouts: 3.52 us -> 9.36 us
    psum x1, waiting for transfers between devices: 86.6 us -> 95.8 us  [shards(): lax.psum(branch_tan.astype(jnp.bfloat16), TENSOR).astype(jnp.float32)]
    all_gather x1, waiting for transfers between devices: 97.1 us -> 88.8 us  [in_one_piece(): filled, at, outs = (lax.all_gather(both, axis, axis=dim, tiled=True), 0, [])]
    all_gather x1, waiting for transfers between devices: 58.1 us -> 63.8 us  [shards(): lax.all_gather(down_weight, axis_name=DP)]
  transfers between devices with their start and end apart: 4 -> 4, of which waited for: 4 -> 4; matrix products, arithmetic and copies ran while one was open for 4% -> 3% of each run, Pallas kernels for 0% -> 0%
where the time goes in v1:
time: 411 us
  waiting for transfers between devices  306 us (74%)
  blocking collectives  42.2 us (10%)
  matrix products  25.4 us (6%)
  between operations  17.2 us (4%)
  other arithmetic  9.77 us (2%)
  local copies, waits for them, and re-layouts  9.36 us (2%)
    psum x1, waiting for transfers between devices, shards(): lax.psum(branch_tan.astype(jnp.bfloat16), TENSOR).astype(jnp.float32)  95.8 us
    all_gather x1, waiting for transfers between devices, in_one_piece(): filled, at, outs = (lax.all_gather(both, axis, axis=dim, tiled=True), 0, [])  88.8 us
    all_gather x1, waiting for transfers between devices, shards(): lax.all_gather(down_weight, axis_name=DP)  63.8 us
    reduce_scatter x1, waiting for transfers between devices, shards(): lax.psum_scatter(lax.optimization_barrier(product.astype(jnp.bfloat16)).a...  57.1 us
    psum x5, blocking collectives, one_axis_at_a_time(): value = lax.psum(value, axis)  42.2 us
    dot_general x3, matrix products, shards(): jnp.dot(columns, piece, preferred_element_type=jnp.float32)  13.2 us
  transfers between devices with their start and end apart: 4, of which 4 were waited for; matrix products, arithmetic and copies ran while one was open for 3% of the time, Pallas kernels for 0%

profile of v1, /device:TPU:2, one launch (start us, length us, event | category | flops | bytes accessed | tf_op | source)
XLA Modules:
  0.0 410.5 jit_solution(14921401980029420283)
XLA Ops:
  7.2 0.0 all-gather.6.cloned.1.call-start
  7.2 0.7 all-gather.6.cloned.1.call-update
  7.9 0.0 all-gather.4.cloned.1.call-start
  7.9 1.9 pad_maximum_fusion
  9.8 0.0 all-gather.4.cloned.1.call-update
  9.8 0.0 all-reduce.8.cloned.1.call-start
  9.9 1.7 fusion.6
  11.5 63.8 %all-gather.6.cloned.1.call-done = bf16[28672,80]{0,1:T(8,128)(2,1)} async-done(((bf16[896,80]{0,1:T(8,128)(2,1)}), bf16[28672,80]{0,1:T(8,128)(2,1)}) %all-gather.6.cloned.1.call-update) | async-done | bytes 4587536 | tf_op jit(solution)/shard_map/all_gather | solution.py:55
  75.4 3.0 copy.13
  78.4 0.0 copy-start
  78.4 0.0 copy-start.7
  78.5 3.7 copy.12
  82.2 88.8 %all-gather.4.cloned.1.call-done = bf16[2560,2688]{1,0:T(8,128)(2,1)} async-done(((bf16[80,2688]{1,0:T(8,128)(2,1)}), bf16[2560,2688]{1,0:T(8,128)(2,1)}) %all-gather.4.cloned.1.call-update) | async-done | bytes 13762576 | tf_op jit(solution)/shard_map/all_gather | solution.py:14
  171.0 0.0 copy-done
  171.0 0.0 copy-done.7
  171.0 3.9 fusion
  174.9 0.0 slice-start
  174.9 4.0 fusion.4
  179.0 0.0 copy-start.2
  179.0 0.0 slice-start.1
  179.0 5.3 %multiply_convert_fusion.2 = (bf16[256,896]{1,0:T(8,128)(2,1)S(1)}, bf16[256,896]{1,0:T(8,128)(2,1)S(1)}, f32[256,896]{1,0:T(8,128)}) fusion(f32[256,896]{1,0:T(8,128)S(1)} %fusion.4, f32[256,896]{1,0:T(8,128)S(1)} %fusion, bf16[2560,2688]{1,0:T(8,128)(2,1)} %all-gather.4.cloned.1.call-done, bf16[256,2560]{1,0:T(8,128)(2,1)S(1)} %copy-done, ...), kind=kOutput, calls=%fused_computation.39 | convolution fusion | flops 1180008448 | bytes 9579520 | tf_op jit(solution)/shard_map/dot_general | solution.py:48
  184.3 0.0 copy-done.2
  184.3 0.0 slice-done
  184.3 0.0 slice-done.1
  184.3 3.2 convolution_convert_fusion.1
  187.5 1.7 fusion.34
  189.2 0.0 all-reduce.8.cloned.1.call-update
  189.2 0.2 reduce-scatter.2.cloned.1.call-start
  190.2 0.0 copy-done.6
  190.3 0.1 select_reduce_fusion
  190.4 95.8 %all-reduce.8.cloned.1.call-done = (bf16[256,2560]{1,0:T(8,128)(2,1)}, bf16[256,2560]{1,0:T(8,128)(2,1)}) async-done(((bf16[256,2560]{1,0:T(8,128)(2,1)}, bf16[256,2560]{1,0:T(8,128)(2,1)}), (bf16[256,2560]{1,0:T(8,128)(2,1)}, bf16[256,2560]{1,0:T(8,128)(2,1)})) %all-reduce.8.cloned.1.call-update) | async-done | bytes 2621456 | tf_op jit(solution)/shard_map/psum | solution.py:65
  286.1 2.5 fusion.11
  288.7 5.3 %fusion.12 = f32[512,896]{1,0:T(8,128)S(1)} fusion(bf16[896,2560]{0,1:T(8,128)(2,1)} %bitcast.14, bf16[256,2560]{1,0:T(8,128)(2,1)S(1)} %get-tuple-element.21, bf16[256,2560]{1,0:T(8,128)(2,1)S(1)} %get-tuple-element.20), kind=kOutput, calls=%fused_computation.17 | convolution fusion | flops 2354053120 | bytes 9043968 | tf_op jit(solution)/shard_map/dot_general | solution.py:71
  294.0 0.0 copy-start.8
  294.0 0.0 copy-done.3
  294.0 0.0 copy-done.4
  294.0 1.3 multiply_reduce_fusion
  295.3 3.7 convolution_convert_fusion
  299.0 0.0 reduce-scatter.2.cloned.1.call-update
  299.1 0.9 copy-done.5
  299.9 0.7 multiply_reduce_fusion.1
  300.6 12.9 %all-reduce.2 = (f32[]{:T(128)}, f32[]{:T(128)}) all-reduce(f32[]{:T(128)} %get-tuple-element.14, f32[]{:T(128)} %multiply_reduce_fusion.1), channel_id=1, replica_groups=mesh['dp_0'=4,'dp_1'=4,'dp_2'=2,'tensor_0'=2,'tensor_1'=4] {'dp_0'}, use_global_device_ids=true, to_apply=%region_6.7 | all-reduce | flops 2 | bytes 16 | tf_op jit(solution)/shard_map/psum | solution.py:23
  313.5 11.1 %all-reduce.1 = (f32[]{:T(128)}, f32[]{:T(128)}) all-reduce(f32[]{:T(128)} %get-tuple-element.6, f32[]{:T(128)} %get-tuple-element.7), channel_id=1, replica_groups=mesh['dp_0'=4,'dp_1'=4,'dp_2'=2,'tensor_0'=2,'tensor_1'=4] {'dp_1'}, use_global_device_ids=true, to_apply=%region_7.8 | all-reduce | flops 2 | bytes 16 | tf_op jit(solution)/shard_map/psum | solution.py:23
  324.6 3.1 all-reduce.4
  327.6 5.5 %all-reduce.3 = (f32[]{:T(128)}, f32[]{:T(128)}) all-reduce(f32[]{:T(128)} %get-tuple-element.10, f32[]{:T(128)} %get-tuple-element.11), channel_id=1, replica_groups=mesh['dp_0'=4,'dp_1'=4,'dp_2'=2,'tensor_0'=2,'tensor_1'=4] {'tensor_0'}, use_global_device_ids=true, to_apply=%region_9.10 | all-reduce | flops 2 | bytes 16 | tf_op jit(solution)/shard_map/psum | solution.py:23
  333.2 9.6 %all-reduce = (f32[]{:T(128)}, f32[]{:T(128)}) all-reduce(f32[]{:T(128)} %get-tuple-element.8, f32[]{:T(128)} %get-tuple-element.9), channel_id=1, replica_groups=mesh['dp_0'=4,'dp_1'=4,'dp_2'=2,'tensor_0'=2,'tensor_1'=4] {'tensor_1'}, use_global_device_ids=true, to_apply=%region_10.11 | all-reduce | flops 2 | bytes 16 | tf_op jit(solution)/shard_map/psum | solution.py:23
  344.2 57.1 %reduce-scatter.2.cloned.1.call-done = bf16[80,896]{1,0:T(8,128)(2,1)} async-done(((bf16[2560,896]{1,0:T(8,128)(2,1)}), bf16[80,896]{1,0:T(8,128)(2,1)}) %reduce-scatter.2.cloned.1.call-update) | async-done | bytes 143376 | tf_op jit(solution)/shard_map/reduce_scatter | solution.py:92
  401.2 1.6 convert_element_type.65
  (11 shorter events, 0.0 us)
Async XLA Ops:
  7.2 68.2 %all-gather.6.cloned.1.call-start = ((), (), s32[]{:S(2)}) async-start(), calls=%async_computation.3 | async-start | bytes 4730880 | tf_op jit(solution)/shard_map/all_gather | solution.py:55
  7.9 163.1 %all-gather.4.cloned.1.call-start = ((), (), s32[]{:S(2)}) async-start(), calls=%async_computation.1 | async-start | bytes 14192640 | tf_op jit(solution)/shard_map/all_gather | solution.py:14
  9.8 276.3 %all-reduce.8.cloned.1.call-start = ((), (), s32[]{:S(2)}) async-start(), calls=%async_computation.4 | async-start | bytes 5242880 | tf_op jit(solution)/shard_map/psum | solution.py:65
  78.4 92.6 %copy-start = (bf16[256,2560]{1,0:T(8,128)(2,1)S(1)}, bf16[256,2560]{1,0:T(8,128)(2,1)}, u32[]{:S(2)}) copy-start(bf16[256,2560]{1,0:T(8,128)(2,1)} %param.9) | copy-start | bytes 3932164
  78.4 92.6 %copy-start.7 = (f32[2560]{0:T(1024)S(1)}, f32[2560]{0:T(1024)}, u32[]{:S(2)}) copy-start(f32[2560]{0:T(1024)} %param.11) | copy-start | bytes 30724
  174.9 9.3 %slice-start = ((s8[4587520]{0:T(1024)(128)(4,1)}), s8[4194304]{0:T(1024)(128)(4,1)S(1)}, s32[]{:S(2)}) async-start(s8[4587520]{0:T(1024)(128)(4,1)} %bitcast.15), calls=%async_computation.5 | async-start | bytes 8388608
  179.0 5.3 %copy-start.2 = (f32[256,896]{1,0:T(8,128)}, f32[256,896]{1,0:T(8,128)S(1)}, u32[]{:S(2)}) copy-start(f32[256,896]{1,0:T(8,128)S(1)} %fusion.4) | copy-start | bytes 2752516
  179.0 5.3 %slice-start.1 = ((s8[4587520]{0:T(1024)(128)(4,1)}), s8[393216]{0:T(1024)(128)(4,1)S(1)}, s32[]{:S(2)}) async-start(s8[4587520]{0:T(1024)(128)(4,1)} %bitcast.15), calls=%async_computation.6 | async-start | bytes 786432
  189.2 1.1 copy-start.6
  189.2 96.9 %copy-start.1 = (bf16[256,2560]{1,0:T(8,128)(2,1)S(1)}, bf16[256,2560]{1,0:T(8,128)(2,1)}, u32[]{:S(2)}) copy-start(bf16[256,2560]{1,0:T(8,128)(2,1)} %param.10) | copy-start | bytes 3932164
  189.2 212.1 %reduce-scatter.2.cloned.1.call-start = ((), (), s32[]{:S(2)}) async-start(), calls=%async_computation.2 | async-start | bytes 4730880 | tf_op jit(solution)/shard_map/reduce_scatter | solution.py:92
  288.6 5.3 %copy-start.3 = (f32[256,896]{1,0:T(8,128)S(1)}, f32[256,896]{1,0:T(8,128)}, u32[]{:S(2)}) copy-start(f32[256,896]{1,0:T(8,128)} %copy-done.2) | copy-start | bytes 2752516
  288.7 5.3 %copy-start.4 = (f32[256,896]{1,0:T(8,128)S(1)}, f32[256,896]{1,0:T(8,128)}, u32[]{:S(2)}) copy-start(f32[256,896]{1,0:T(8,128)} %get-tuple-element.22) | copy-start | bytes 2752516
  294.0 1.3 copy-start.8
  299.0 0.9 copy-start.5
Sparse Core Ops, SparseCore 0:
  10.6 64.7 all-gather.5
  78.0 92.9 all-gather.3
  189.3 96.7 all-reduce.7
  299.2 102.0 reduce-scatter.1
